TPU v7x, 32 devices: a whole 2x2x4 slice. The times are simulated.
32 devices in a mesh: dom: 8 (over z, x), sub: 4 (over y, core).
Axes of the slice: x: 2, y: 2, z: 4, core: 2. Of those that a mesh axis runs over, the one named last changes fastest.
Arguments:
- level_set: float32 [64, 32, 128], P('dom', 'sub'), may hold values from 0 to 1
- velocity: float32 [3, 64, 32, 128], P(None, 'dom', 'sub'), may hold values from -6 to 6
- source: float32 [64, 32, 128], P('dom', 'sub'), may hold values from -12 to 12
Outputs:
- new_level: float32 [64, 32, 128], P('dom', 'sub')
- pressure: float32 [64, 32, 128], P('dom', 'sub')
- correction: float32 [64, 32, 128], P('dom', 'sub')
All inputs are finite; a program needn't handle non-finite values.
Results may differ from a plain program's by a relative error of at most 0.0003.
Values sent between devices are 32-bit elements; how exact they have to be, the bound alone decides.
A program may use at most 64 MiB of HBM per device.

v0:
```python
import math
import jax
import jax.numpy as jnp
import numpy as np
from jax import lax
from jax.sharding import PartitionSpec as P

SWEEPS = 2
PITERS = 2
gll_nodes = [
    -1.0,
    -0.8717401485096066,
    -0.5917001814331423,
    -0.2092992179024789,
    0.2092992179024789,
    0.5917001814331423,
    0.8717401485096066,
    1.0,
]
advect_step = 0.05
reinit_step = 0.02
interface_width = 0.1
density_ratio = 9.0


def padded(x, sides, width):
    for axis, dim in sides:
        devices, length = (lax.axis_size(axis), x.shape[dim])
        up = [(i, (i + 1) % devices) for i in range(devices)]
        down = [(j, i) for i, j in up]
        last = lax.slice_in_dim(x, length - width, length, axis=dim)
        leading = lax.slice_in_dim(x, 0, width, axis=dim)
        before = lax.ppermute(last, axis, up)
        after = lax.ppermute(leading, axis, down)
        x = jnp.concatenate([before, x, after], axis=dim)
    return x


def tables():
    node_points = np.array(gll_nodes)
    poly_order = 7
    values_prev = np.ones(8)
    values_now = node_points.copy()
    for degree in range(1, poly_order):
        values_next = ((2 * degree + 1) * node_points * values_now - degree * values_prev) / (
            degree + 1
        )
        values_prev, values_now = (values_now, values_next)
    matrix = np.zeros((8, 8))
    for line in range(8):
        for column in range(8):
            if line != column:
                matrix[line, column] = values_now[line] / (
                    values_now[column] * (node_points[line] - node_points[column])
                )
    matrix[0, 0] = -poly_order * (poly_order + 1) / 4.0
    matrix[7, 7] = poly_order * (poly_order + 1) / 4.0
    weights = 2.0 / (poly_order * (poly_order + 1) * values_now**2)
    return (matrix, weights)


def point_tables(full_shape, weights):
    corner_count = np.array([2.0, 1.0, 1.0, 1.0, 1.0, 1.0, 1.0, 2.0])
    weight_lines = []
    count_lines = []
    for dim_index in (1, 2, 3):
        repeats = full_shape[dim_index] // 8
        weight_lines.append(jnp.asarray(np.tile(weights, repeats), jnp.float32))
        count_lines.append(jnp.asarray(np.tile(1.0 / corner_count, repeats), jnp.float32))
    weight_cube = (
        weight_lines[0][:, None, None]
        * weight_lines[1][None, :, None]
        * weight_lines[2][None, None, :]
    )[None]
    inv_mult = (
        count_lines[0][:, None, None]
        * count_lines[1][None, :, None]
        * count_lines[2][None, None, :]
    )[None]
    return (weight_cube, inv_mult)


def derive(values, dim_index, matrix):
    full_shape = values.shape
    highest = lax.Precision.HIGHEST
    if dim_index == 1:
        blocks = values.reshape((full_shape[0], full_shape[1] // 8, 8) + full_shape[2:])
        result = jnp.einsum(
            "baipq,ji->bajpq", blocks, jnp.asarray(matrix, jnp.float32), precision=highest
        )
    elif dim_index == 2:
        blocks = values.reshape(full_shape[:2] + (full_shape[2] // 8, 8, full_shape[3]))
        result = jnp.einsum(
            "bpaiq,ji->bpajq", blocks, jnp.asarray(matrix, jnp.float32), precision=highest
        )
    else:
        block_width = math.gcd(full_shape[3], 128)
        block_matrix = jnp.asarray(np.kron(np.eye(block_width // 8), matrix), jnp.float32)
        blocks = values.reshape(full_shape[:3] + (full_shape[3] // block_width, block_width))
        result = jnp.einsum("bpqai,ji->bpqaj", blocks, block_matrix, precision=highest)
    return result.reshape(full_shape)


def gradient(values, matrix):
    return [derive(values, 1, matrix), derive(values, 2, matrix), derive(values, 3, matrix)]


def join_edges(values, upper, lower, dim_index):
    position = lax.broadcasted_iota(jnp.int32, values.shape, dim_index) % 8
    return values + jnp.where(position == 7, upper, 0.0) + jnp.where(position == 0, lower, 0.0)


def fold_faces(widened, dim_index, length):
    values = lax.slice_in_dim(widened, 1, length + 1, axis=dim_index)
    upper = lax.slice_in_dim(widened, 2, length + 2, axis=dim_index)
    lower = lax.slice_in_dim(widened, 0, length, axis=dim_index)
    return join_edges(values, upper, lower, dim_index)


def fold_local(values, dim_index):
    upper = jnp.roll(values, -1, axis=dim_index)
    lower = jnp.roll(values, 1, axis=dim_index)
    return join_edges(values, upper, lower, dim_index)


def assemble(values):
    widened = padded(values, (("dom", 1),), 1)
    values = fold_faces(widened, 1, values.shape[1])
    widened = padded(values, (("sub", 2),), 1)
    values = fold_faces(widened, 2, values.shape[2])
    return fold_local(values, 3)


def both_sums(residual, precond, applied, inv_mult):
    return lax.psum(
        (jnp.sum(residual * precond * inv_mult), jnp.sum(precond * applied * inv_mult)),
        ("dom", "sub"),
    )


def local(level_set, velocity, source):
    matrix, weights = tables()
    phase_field = level_set[None]
    weight_cube, inv_mult = point_tables(phase_field.shape, weights)
    gradients = gradient(phase_field, matrix)
    advected = phase_field - advect_step * (
        velocity[0:1] * gradients[0] + velocity[1:2] * gradients[1] + velocity[2:3] * gradients[2]
    )
    phase_field = assemble(advected) * inv_mult
    gradients = gradient(phase_field, matrix)
    magnitude = jnp.sqrt(
        gradients[0] * gradients[0] + gradients[1] * gradients[1] + gradients[2] * gradients[2]
    )
    scaled = 1.0 / jnp.maximum(magnitude, 1.0)
    normals = [gradients[0] * scaled, gradients[1] * scaled, gradients[2] * scaled]
    for sweep_index in range(SWEEPS):
        if sweep_index > 0:
            gradients = gradient(phase_field, matrix)
        compress = phase_field * (1.0 - phase_field)
        change = derive(interface_width * gradients[0] - compress * normals[0], 1, matrix)
        change = change + derive(interface_width * gradients[1] - compress * normals[1], 2, matrix)
        change = change + derive(interface_width * gradients[2] - compress * normals[2], 3, matrix)
        phase_field = phase_field + reinit_step * assemble(change) * inv_mult
    mobility = 1.0 / (1.0 + density_ratio * phase_field * phase_field)
    weighted = weight_cube * mobility
    square_t = (matrix * matrix).T
    diag_local = (
        weight_cube
        + derive(weighted, 1, square_t)
        + derive(weighted, 2, square_t)
        + derive(weighted, 3, square_t)
    )
    assembled = assemble(jnp.concatenate([weight_cube * source[None], diag_local], axis=0))
    right_side = assembled[0:1]
    diagonal = assembled[1:2]
    transposed = matrix.T

    def operate(direction):
        grads_dir = gradient(direction, matrix)
        local_sum = weight_cube * direction + derive(weighted * grads_dir[0], 1, transposed)
        local_sum = (
            local_sum
            + derive(weighted * grads_dir[1], 2, transposed)
            + derive(weighted * grads_dir[2], 3, transposed)
        )
        return assemble(local_sum)

    solution = jnp.zeros_like(right_side)
    residual = right_side
    precond = residual / diagonal
    applied = operate(precond)
    norm_now, product = both_sums(residual, precond, applied, inv_mult)
    step_size = norm_now / product
    direction = precond
    along_image = applied
    for step_index in range(PITERS):
        solution = solution + step_size * direction
        residual = residual - step_size * along_image
        if step_index + 1 < PITERS:
            precond = residual / diagonal
            applied = operate(precond)
            norm_next, product = both_sums(residual, precond, applied, inv_mult)
            ratio_new = norm_next / norm_now
            step_size = norm_next / (product - ratio_new * norm_next / step_size)
            direction = precond + ratio_new * direction
            along_image = applied + ratio_new * along_image
            norm_now = norm_next
    return (phase_field[0], solution[0], (residual / diagonal)[0])


def solution(mesh):
    return jax.shard_map(
        local,
        mesh=mesh,
        in_specs=(P("dom", "sub", None), P(None, "dom", "sub", None), P("dom", "sub", None)),
        out_specs=(P("dom", "sub", None), P("dom", "sub", None), P("dom", "sub", None)),
        check_vma=False,
    )
```

profile of v0, /device:TPU:14, one launch (start us, length us, event | category | flops | bytes accessed | tf_op | source)
XLA Modules:
  0.0 165.5 jit_solution(13758522378719981348)
XLA Ops:
  0.7 0.8 fusion.168
  1.8 0.7 copy-done
  2.8 0.6 collective-permute-start
  3.3 2.4 %collective-permute-start.1 = (f32[1,1,8,128]{3,1,2,0:T(1,128)S(1)}, f32[1,1,8,128]{3,1,2,0:T(1,128)S(1)}, u32[]{:S(2)}, u32[]{:S(2)}) collective-permute-start(f32[1,1,8,128]{3,1,2,0:T(1,128)S(1)} %get-tuple-element.74), channel_id=1, source_target_pairs={{0,4},{4,8},{8,12},{12,16},{16,20},{20,24},{24,28},{28,0},{1,5},{5... | collective-permute-start | bytes 12296 | tf_op jit(solution)/shard_map/ppermute | solution.py:33
  5.7 0.6 copy-done.10
  6.5 0.8 collective-permute-done
  7.5 0.5 collective-permute-start.3
  8.0 0.8 collective-permute-done.2
  8.8 1.8 %collective-permute-done.3 = f32[1,8,1,128]{3,1,2,0:T(8,128)S(1)} collective-permute-done((f32[1,8,1,128]{3,1,2,0:T(8,128)S(1)}, f32[1,8,1,128]{3,1,2,0:T(8,128)S(1)}, u32[]{:S(2)}, u32[]{:S(2)}) %collective-permute-start.3) | collective-permute-done | bytes 4128 | tf_op jit(solution)/shard_map/ppermute | solution.py:33
  10.8 0.7 copy-done.6
  12.8 2.0 %collective-permute-start.4 = (f32[1,1,8,128]{3,1,2,0:T(1,128)S(1)}, f32[1,1,8,128]{3,1,2,0:T(1,128)S(1)}, u32[]{:S(2)}, u32[]{:S(2)}) collective-permute-start(f32[1,1,8,128]{3,1,2,0:T(1,128)S(1)} %get-tuple-element.61), channel_id=1, source_target_pairs={{4,0},{8,4},{12,8},{16,12},{20,16},{24,20},{28,24},{0,28},{5,1},{9... | collective-permute-start | bytes 12296 | tf_op jit(solution)/shard_map/ppermute | solution.py:34
  14.8 1.1 collective-permute-start.5
  15.9 1.5 collective-permute-done.4
  17.4 1.1 collective-permute-done.5
  18.7 0.5 collective-permute-start.7
  19.2 0.8 collective-permute-done.6
  20.0 1.8 %collective-permute-done.7 = f32[1,8,1,128]{3,1,2,0:T(8,128)S(1)} collective-permute-done((f32[1,8,1,128]{3,1,2,0:T(8,128)S(1)}, f32[1,8,1,128]{3,1,2,0:T(8,128)S(1)}, u32[]{:S(2)}, u32[]{:S(2)}) %collective-permute-start.7) | collective-permute-done | bytes 4128 | tf_op jit(solution)/shard_map/ppermute | solution.py:33
  23.4 4.8 %collective-permute-start.8 = (f32[1,1,8,128]{3,1,2,0:T(1,128)S(1)}, f32[1,1,8,128]{3,1,2,0:T(1,128)S(1)}, u32[]{:S(2)}, u32[]{:S(2)}) collective-permute-start(f32[1,1,8,128]{3,1,2,0:T(1,128)S(1)} %get-tuple-element.53), channel_id=1, source_target_pairs={{4,0},{8,4},{12,8},{16,12},{20,16},{24,20},{28,24},{0,28},{5,1},{9... | collective-permute-start | bytes 12296 | tf_op jit(solution)/shard_map/ppermute | solution.py:34
  28.2 1.2 collective-permute-done.8
  29.5 2.3 %collective-permute-done.9 = f32[1,1,8,128]{3,1,2,0:T(1,128)S(1)} collective-permute-done((f32[1,1,8,128]{3,1,2,0:T(1,128)S(1)}, f32[1,1,8,128]{3,1,2,0:T(1,128)S(1)}, u32[]{:S(2)}, u32[]{:S(2)}) %collective-permute-start.9) | collective-permute-done | bytes 4128 | tf_op jit(solution)/shard_map/ppermute | solution.py:33
  32.6 0.7 collective-permute-done.10
  33.3 1.8 %collective-permute-done.11 = f32[1,8,1,128]{3,1,2,0:T(8,128)S(1)} collective-permute-done((f32[1,8,1,128]{3,1,2,0:T(8,128)S(1)}, f32[1,8,1,128]{3,1,2,0:T(8,128)S(1)}, u32[]{:S(2)}, u32[]{:S(2)}) %collective-permute-start.11) | collective-permute-done | bytes 4128 | tf_op jit(solution)/shard_map/ppermute | solution.py:33
  35.4 0.5 copy-done.8
  36.4 0.6 copy-done.11
  37.3 3.0 %collective-permute-start.12 = (f32[2,1,8,128]{3,1,2,0:T(1,128)S(1)}, f32[2,1,8,128]{3,1,2,0:T(1,128)S(1)}, u32[]{:S(2)}, u32[]{:S(2)}) collective-permute-start(f32[2,1,8,128]{3,1,2,0:T(1,128)S(1)} %get-tuple-element.29), channel_id=1, source_target_pairs={{4,0},{8,4},{12,8},{16,12},{20,16},{24,20},{28,24},{0,28},{5,1},{9... | collective-permute-start | bytes 24584 | tf_op jit(solution)/shard_map/ppermute | solution.py:34
  40.3 1.6 collective-permute-done.12
  41.9 2.0 %collective-permute-done.13 = f32[2,1,8,128]{3,1,2,0:T(1,128)S(1)} collective-permute-done((f32[2,1,8,128]{3,1,2,0:T(1,128)S(1)}, f32[2,1,8,128]{3,1,2,0:T(1,128)S(1)}, u32[]{:S(2)}, u32[]{:S(2)}) %collective-permute-start.13) | collective-permute-done | bytes 8224 | tf_op jit(solution)/shard_map/ppermute | solution.py:33
  44.1 0.5 collective-permute-start.15
  44.6 0.9 collective-permute-done.14
  45.4 1.8 %collective-permute-done.15 = f32[2,8,1,128]{3,1,2,0:T(8,128)S(1)} collective-permute-done((f32[2,8,1,128]{3,1,2,0:T(8,128)S(1)}, f32[2,8,1,128]{3,1,2,0:T(8,128)S(1)}, u32[]{:S(2)}, u32[]{:S(2)}) %collective-permute-start.15) | collective-permute-done | bytes 8224 | tf_op jit(solution)/shard_map/ppermute | solution.py:33
  48.3 0.6 copy-done.4
  49.3 0.7 copy-done.3
  50.2 2.8 %collective-permute-start.16 = (f32[1,1,8,128]{3,1,2,0:T(1,128)S(1)}, f32[1,1,8,128]{3,1,2,0:T(1,128)S(1)}, u32[]{:S(2)}, u32[]{:S(2)}) collective-permute-start(f32[1,1,8,128]{3,1,2,0:T(1,128)S(1)} %get-tuple-element.45), channel_id=1, source_target_pairs={{4,0},{8,4},{12,8},{16,12},{20,16},{24,20},{28,24},{0,28},{5,1},{9... | collective-permute-start | bytes 12296 | tf_op jit(solution)/shard_map/ppermute | solution.py:34
  53.2 1.6 collective-permute-done.16
  54.7 1.9 %collective-permute-done.17 = f32[1,1,8,128]{3,1,2,0:T(1,128)S(1)} collective-permute-done((f32[1,1,8,128]{3,1,2,0:T(1,128)S(1)}, f32[1,1,8,128]{3,1,2,0:T(1,128)S(1)}, u32[]{:S(2)}, u32[]{:S(2)}) %collective-permute-start.17) | collective-permute-done | bytes 4128 | tf_op jit(solution)/shard_map/ppermute | solution.py:33
  57.3 0.8 collective-permute-done.18
  58.1 1.8 %collective-permute-done.19 = f32[1,8,1,128]{3,1,2,0:T(8,128)S(1)} collective-permute-done((f32[1,8,1,128]{3,1,2,0:T(8,128)S(1)}, f32[1,8,1,128]{3,1,2,0:T(8,128)S(1)}, u32[]{:S(2)}, u32[]{:S(2)}) %collective-permute-start.19) | collective-permute-done | bytes 4128 | tf_op jit(solution)/shard_map/ppermute | solution.py:33
  60.1 0.7 fusion.105
  60.8 44.3 %all-reduce.1 = (f32[]{:T(128)}, f32[]{:T(128)}) all-reduce(f32[]{:T(128)} %get-tuple-element.9, f32[]{:T(128)} %get-tuple-element.8), channel_id=1, replica_groups=mesh['dom'=8,'sub'=4] {'dom','sub'}, use_global_device_ids=true, to_apply=%region_1.2 | all-reduce | flops 2 | bytes 16 | tf_op jit(solution)/shard_map/psum | solution.py:135
  107.7 0.6 collective-permute-start.20
  108.4 2.3 %collective-permute-start.21 = (f32[1,1,8,128]{3,1,2,0:T(1,128)S(1)}, f32[1,1,8,128]{3,1,2,0:T(1,128)S(1)}, u32[]{:S(2)}, u32[]{:S(2)}) collective-permute-start(f32[1,1,8,128]{3,1,2,0:T(1,128)S(1)} %get-tuple-element.38), channel_id=1, source_target_pairs={{0,4},{4,8},{8,12},{12,16},{16,20},{20,24},{24,28},{28,0},{1,5},{5... | collective-permute-start | bytes 12296 | tf_op jit(solution)/shard_map/ppermute | solution.py:33
  110.7 1.6 collective-permute-done.20
  113.0 0.6 copy.103
  113.8 1.8 %collective-permute-done.23 = f32[1,8,1,128]{3,1,2,0:T(8,128)S(1)} collective-permute-done((f32[1,8,1,128]{3,1,2,0:T(8,128)S(1)}, f32[1,8,1,128]{3,1,2,0:T(8,128)S(1)}, u32[]{:S(2)}, u32[]{:S(2)}) %collective-permute-start.23) | collective-permute-done | bytes 4128 | tf_op jit(solution)/shard_map/ppermute | solution.py:33
  115.8 0.8 fusion.107
  116.6 43.1 %all-reduce = (f32[]{:T(128)}, f32[]{:T(128)}) all-reduce(f32[]{:T(128)} %get-tuple-element.7, f32[]{:T(128)} %get-tuple-element.6), channel_id=1, replica_groups=mesh['dom'=8,'sub'=4] {'dom','sub'}, use_global_device_ids=true, to_apply=%region_5.6 | all-reduce | flops 2 | bytes 16 | tf_op jit(solution)/shard_map/psum | solution.py:135
  164.3 0.6 copy.105
  164.9 0.6 copy.104
  (120 shorter events, 11.2 us)
Async XLA Ops:
  0.6 0.8 copy-start.1
  0.6 0.8 copy-start.2
  1.6 0.9 copy-start
  2.8 4.6 %collective-permute-start = (f32[1,1,8,128]{3,1,2,0:T(1,128)S(1)}, f32[1,1,8,128]{3,1,2,0:T(1,128)S(1)}, u32[]{:S(2)}, u32[]{:S(2)}) collective-permute-start(f32[1,1,8,128]{3,1,2,0:T(1,128)S(1)} %get-tuple-element.73), channel_id=1, source_target_pairs={{4,0},{8,4},{12,8},{16,12},{20,16},{24,20},{28,24},{0,28},{5,1},{9... | collective-permute-start | bytes 12296 | tf_op jit(solution)/shard_map/ppermute | solution.py:34
  3.3 4.0 %collective-permute-start.1 = (f32[1,1,8,128]{3,1,2,0:T(1,128)S(1)}, f32[1,1,8,128]{3,1,2,0:T(1,128)S(1)}, u32[]{:S(2)}, u32[]{:S(2)}) collective-permute-start(f32[1,1,8,128]{3,1,2,0:T(1,128)S(1)} %get-tuple-element.74), channel_id=1, source_target_pairs={{0,4},{4,8},{8,12},{12,16},{16,20},{20,24},{24,28},{28,0},{1,5},{5... | collective-permute-start | bytes 12296 | tf_op jit(solution)/shard_map/ppermute | solution.py:33
  5.7 0.7 copy-start.10
  7.4 1.4 collective-permute-start.2
  7.5 3.1 %collective-permute-start.3 = (f32[1,8,1,128]{3,1,2,0:T(8,128)S(1)}, f32[1,8,1,128]{3,1,2,0:T(8,128)S(1)}, u32[]{:S(2)}, u32[]{:S(2)}) collective-permute-start(f32[1,8,1,128]{3,1,2,0:T(8,128)S(1)} %get-tuple-element.72), channel_id=1, source_target_pairs={{0,1},{1,2},{2,3},{3,0},{4,5},{5,6},{6,7},{7,4},{8,9},{9,10},{10,1... | collective-permute-start | bytes 12296 | tf_op jit(solution)/shard_map/ppermute | solution.py:33
  10.8 0.7 copy-start.6
  12.8 4.6 %collective-permute-start.4 = (f32[1,1,8,128]{3,1,2,0:T(1,128)S(1)}, f32[1,1,8,128]{3,1,2,0:T(1,128)S(1)}, u32[]{:S(2)}, u32[]{:S(2)}) collective-permute-start(f32[1,1,8,128]{3,1,2,0:T(1,128)S(1)} %get-tuple-element.61), channel_id=1, source_target_pairs={{4,0},{8,4},{12,8},{16,12},{20,16},{24,20},{28,24},{0,28},{5,1},{9... | collective-permute-start | bytes 12296 | tf_op jit(solution)/shard_map/ppermute | solution.py:34
  14.8 3.7 %collective-permute-start.5 = (f32[1,1,8,128]{3,1,2,0:T(1,128)S(1)}, f32[1,1,8,128]{3,1,2,0:T(1,128)S(1)}, u32[]{:S(2)}, u32[]{:S(2)}) collective-permute-start(f32[1,1,8,128]{3,1,2,0:T(1,128)S(1)} %get-tuple-element.62), channel_id=1, source_target_pairs={{0,4},{4,8},{8,12},{12,16},{16,20},{20,24},{24,28},{28,0},{1,5},{5... | collective-permute-start | bytes 12296 | tf_op jit(solution)/shard_map/ppermute | solution.py:33
  18.6 1.4 collective-permute-start.6
  18.7 3.1 %collective-permute-start.7 = (f32[1,8,1,128]{3,1,2,0:T(8,128)S(1)}, f32[1,8,1,128]{3,1,2,0:T(8,128)S(1)}, u32[]{:S(2)}, u32[]{:S(2)}) collective-permute-start(f32[1,8,1,128]{3,1,2,0:T(8,128)S(1)} %get-tuple-element.60), channel_id=1, source_target_pairs={{0,1},{1,2},{2,3},{3,0},{4,5},{5,6},{6,7},{7,4},{8,9},{9,10},{10,1... | collective-permute-start | bytes 12296 | tf_op jit(solution)/shard_map/ppermute | solution.py:33
  23.4 4.8 %copy-start.9 = (f32[8]{0:T(128)S(1)}, f32[8]{0:T(128)}, u32[]{:S(2)}) copy-start(f32[8]{0:T(128)} %constant.109.clone) | copy-start | bytes 100
  23.4 6.1 %collective-permute-start.8 = (f32[1,1,8,128]{3,1,2,0:T(1,128)S(1)}, f32[1,1,8,128]{3,1,2,0:T(1,128)S(1)}, u32[]{:S(2)}, u32[]{:S(2)}) collective-permute-start(f32[1,1,8,128]{3,1,2,0:T(1,128)S(1)} %get-tuple-element.53), channel_id=1, source_target_pairs={{4,0},{8,4},{12,8},{16,12},{20,16},{24,20},{28,24},{0,28},{5,1},{9... | collective-permute-start | bytes 12296 | tf_op jit(solution)/shard_map/ppermute | solution.py:34
  28.2 3.6 %collective-permute-start.9 = (f32[1,1,8,128]{3,1,2,0:T(1,128)S(1)}, f32[1,1,8,128]{3,1,2,0:T(1,128)S(1)}, u32[]{:S(2)}, u32[]{:S(2)}) collective-permute-start(f32[1,1,8,128]{3,1,2,0:T(1,128)S(1)} %get-tuple-element.54), channel_id=1, source_target_pairs={{0,4},{4,8},{8,12},{12,16},{16,20},{20,24},{24,28},{28,0},{1,5},{5... | collective-permute-start | bytes 12296 | tf_op jit(solution)/shard_map/ppermute | solution.py:33
  28.2 4.2 %copy-start.5 = (f32[8,8,128]{2,1,0:T(8,128)S(1)}, f32[8,8,128]{2,1,0:T(8,128)}, u32[]{:S(2)}) copy-start(f32[8,8,128]{2,1,0:T(8,128)} %param.41) | copy-start | bytes 98308
  31.9 0.7 copy-start.7
  31.9 1.4 collective-permute-start.10
  31.9 3.1 %collective-permute-start.11 = (f32[1,8,1,128]{3,1,2,0:T(8,128)S(1)}, f32[1,8,1,128]{3,1,2,0:T(8,128)S(1)}, u32[]{:S(2)}, u32[]{:S(2)}) collective-permute-start(f32[1,8,1,128]{3,1,2,0:T(8,128)S(1)} %get-tuple-element.52), channel_id=1, source_target_pairs={{0,1},{1,2},{2,3},{3,0},{4,5},{5,6},{6,7},{7,4},{8,9},{9,10},{10,1... | collective-permute-start | bytes 12296 | tf_op jit(solution)/shard_map/ppermute | solution.py:33
  35.3 0.7 copy-start.8
  36.1 0.9 copy-start.11
  37.3 4.6 %collective-permute-start.12 = (f32[2,1,8,128]{3,1,2,0:T(1,128)S(1)}, f32[2,1,8,128]{3,1,2,0:T(1,128)S(1)}, u32[]{:S(2)}, u32[]{:S(2)}) collective-permute-start(f32[2,1,8,128]{3,1,2,0:T(1,128)S(1)} %get-tuple-element.29), channel_id=1, source_target_pairs={{4,0},{8,4},{12,8},{16,12},{20,16},{24,20},{28,24},{0,28},{5,1},{9... | collective-permute-start | bytes 24584 | tf_op jit(solution)/shard_map/ppermute | solution.py:34
  40.3 3.7 %collective-permute-start.13 = (f32[2,1,8,128]{3,1,2,0:T(1,128)S(1)}, f32[2,1,8,128]{3,1,2,0:T(1,128)S(1)}, u32[]{:S(2)}, u32[]{:S(2)}) collective-permute-start(f32[2,1,8,128]{3,1,2,0:T(1,128)S(1)} %get-tuple-element.30), channel_id=1, source_target_pairs={{0,4},{4,8},{8,12},{12,16},{16,20},{20,24},{24,28},{28,0},{1,5},{5... | collective-permute-start | bytes 24584 | tf_op jit(solution)/shard_map/ppermute | solution.py:33
  44.0 1.4 collective-permute-start.14
  44.1 3.1 %collective-permute-start.15 = (f32[2,8,1,128]{3,1,2,0:T(8,128)S(1)}, f32[2,8,1,128]{3,1,2,0:T(8,128)S(1)}, u32[]{:S(2)}, u32[]{:S(2)}) collective-permute-start(f32[2,8,1,128]{3,1,2,0:T(8,128)S(1)} %get-tuple-element.28), channel_id=1, source_target_pairs={{0,1},{1,2},{2,3},{3,0},{4,5},{5,6},{6,7},{7,4},{8,9},{9,10},{10,1... | collective-permute-start | bytes 24584 | tf_op jit(solution)/shard_map/ppermute | solution.py:33
  48.2 0.7 copy-start.4
  49.1 0.8 copy-start.3
  50.2 4.6 %collective-permute-start.16 = (f32[1,1,8,128]{3,1,2,0:T(1,128)S(1)}, f32[1,1,8,128]{3,1,2,0:T(1,128)S(1)}, u32[]{:S(2)}, u32[]{:S(2)}) collective-permute-start(f32[1,1,8,128]{3,1,2,0:T(1,128)S(1)} %get-tuple-element.45), channel_id=1, source_target_pairs={{4,0},{8,4},{12,8},{16,12},{20,16},{24,20},{28,24},{0,28},{5,1},{9... | collective-permute-start | bytes 12296 | tf_op jit(solution)/shard_map/ppermute | solution.py:34
  53.0 3.6 %collective-permute-start.17 = (f32[1,1,8,128]{3,1,2,0:T(1,128)S(1)}, f32[1,1,8,128]{3,1,2,0:T(1,128)S(1)}, u32[]{:S(2)}, u32[]{:S(2)}) collective-permute-start(f32[1,1,8,128]{3,1,2,0:T(1,128)S(1)} %get-tuple-element.46), channel_id=1, source_target_pairs={{0,4},{4,8},{8,12},{12,16},{16,20},{20,24},{24,28},{28,0},{1,5},{5... | collective-permute-start | bytes 12296 | tf_op jit(solution)/shard_map/ppermute | solution.py:33
  56.7 1.4 collective-permute-start.18
  56.8 3.1 %collective-permute-start.19 = (f32[1,8,1,128]{3,1,2,0:T(8,128)S(1)}, f32[1,8,1,128]{3,1,2,0:T(8,128)S(1)}, u32[]{:S(2)}, u32[]{:S(2)}) collective-permute-start(f32[1,8,1,128]{3,1,2,0:T(8,128)S(1)} %get-tuple-element.44), channel_id=1, source_target_pairs={{0,1},{1,2},{2,3},{3,0},{4,5},{5,6},{6,7},{7,4},{8,9},{9,10},{10,1... | collective-permute-start | bytes 12296 | tf_op jit(solution)/shard_map/ppermute | solution.py:33
  107.7 4.6 %collective-permute-start.20 = (f32[1,1,8,128]{3,1,2,0:T(1,128)S(1)}, f32[1,1,8,128]{3,1,2,0:T(1,128)S(1)}, u32[]{:S(2)}, u32[]{:S(2)}) collective-permute-start(f32[1,1,8,128]{3,1,2,0:T(1,128)S(1)} %get-tuple-element.37), channel_id=1, source_target_pairs={{4,0},{8,4},{12,8},{16,12},{20,16},{24,20},{28,24},{0,28},{5,1},{9... | collective-permute-start | bytes 12296 | tf_op jit(solution)/shard_map/ppermute | solution.py:34
  108.4 3.9 %collective-permute-start.21 = (f32[1,1,8,128]{3,1,2,0:T(1,128)S(1)}, f32[1,1,8,128]{3,1,2,0:T(1,128)S(1)}, u32[]{:S(2)}, u32[]{:S(2)}) collective-permute-start(f32[1,1,8,128]{3,1,2,0:T(1,128)S(1)} %get-tuple-element.38), channel_id=1, source_target_pairs={{0,4},{4,8},{8,12},{12,16},{16,20},{20,24},{24,28},{28,0},{1,5},{5... | collective-permute-start | bytes 12296 | tf_op jit(solution)/shard_map/ppermute | solution.py:33
  112.4 1.4 collective-permute-start.22
  112.5 3.1 %collective-permute-start.23 = (f32[1,8,1,128]{3,1,2,0:T(8,128)S(1)}, f32[1,8,1,128]{3,1,2,0:T(8,128)S(1)}, u32[]{:S(2)}, u32[]{:S(2)}) collective-permute-start(f32[1,8,1,128]{3,1,2,0:T(8,128)S(1)} %get-tuple-element.36), channel_id=1, source_target_pairs={{0,1},{1,2},{2,3},{3,0},{4,5},{5,6},{6,7},{7,4},{8,9},{9,10},{10,1... | collective-permute-start | bytes 12296 | tf_op jit(solution)/shard_map/ppermute | solution.py:33
where the time goes:
time: 166 us
  blocking collectives  87.4 us (53%)
  waiting for transfers between devices  30.5 us (18%)
  starting transfers between devices  23.1 us (14%)
  local copies, waits for them, and re-layouts  8.16 us (5%)
  between operations  7.03 us (4%)
  matrix products  5.75 us (3%)
  other arithmetic  3.65 us (2%)
    psum x2, blocking collectives, both_sums(): lax.psum((jnp.sum(residual * precond * inv_mult), jnp.sum(precond * appli...  87.4 us
    ppermute x12, waiting for transfers between devices, padded(): before = lax.ppermute(last, axis, up)  17.9 us
    ppermute x12, starting transfers between devices, padded(): after = lax.ppermute(leading, axis, down)  14.1 us
    ppermute x12, waiting for transfers between devices, padded(): after = lax.ppermute(leading, axis, down)  12.6 us
    ppermute x12, starting transfers between devices, padded(): before = lax.ppermute(last, axis, up)  8.96 us
    unnamed x27, local copies, waits for them, and re-layouts  6.39 us
  transfers between devices with their start and end apart: 24, of which 22 were waited for; matrix products, arithmetic and copies ran while one was open for 1% of the time, Pallas kernels for 0%

commit v1 on v0

--- a/solution.py
+++ b/solution.py
@@ -133,8 +133,10 @@
 
 def both_sums(residual, precond, applied, inv_mult):
     return lax.psum(
-        (jnp.sum(residual * precond * inv_mult), jnp.sum(precond * applied * inv_mult)),
-        ("dom", "sub"),
+        lax.psum(
+            (jnp.sum(residual * precond * inv_mult), jnp.sum(precond * applied * inv_mult)), "dom"
+        ),
+        "sub",
     )
 
 

time: 166 us -> 137 us (0.83)
  the two profiles are of different devices: /device:TPU:14 before, /device:TPU:0 now
where the time goes in v1:
time: 137 us
  blocking collectives  48.2 us (35%)
  waiting for transfers between devices  44.1 us (32%)
  starting transfers between devices  19.8 us (14%)
  local copies, waits for them, and re-layouts  8.15 us (6%)
  between operations  7.11 us (5%)
  matrix products  5.75 us (4%)
  other arithmetic  3.64 us (3%)
    psum x2, blocking collectives, both_sums(): lax.psum((jnp.sum(residual * precond * inv_mult), jnp.sum(precond * appli...  35.6 us
    ppermute x12, waiting for transfers between devices, padded(): before = lax.ppermute(last, axis, up)  31.5 us
    ppermute x12, waiting for transfers between devices, padded(): after = lax.ppermute(leading, axis, down)  12.6 us
    psum x2, blocking collectives, both_sums(): lax.psum(lax.psum((jnp.sum(residual * precond * inv_mult), jnp.sum(precon...  12.6 us
    ppermute x12, starting transfers between devices, padded(): before = lax.ppermute(last, axis, up)  11.1 us
    ppermute x12, starting transfers between devices, padded(): after = lax.ppermute(leading, axis, down)  8.7 us
    unnamed x27, local copies, waits for them, and re-layouts  6.38 us
  transfers between devices with their start and end apart: 24, of which 24 were waited for; matrix products, arithmetic and copies ran while one was open for 1% of the time, Pallas kernels for 0%

profile of v1, /device:TPU:0, one launch (start us, length us, event | category | flops | bytes accessed | tf_op | source)
XLA Modules:
  0.0 136.7 jit_solution(9894822514776414924)
XLA Ops:
  0.7 0.8 fusion.168
  1.8 0.7 copy-done
  2.7 6.1 %collective-permute-start = (f32[1,1,8,128]{3,1,2,0:T(1,128)S(1)}, f32[1,1,8,128]{3,1,2,0:T(1,128)S(1)}, u32[]{:S(2)}, u32[]{:S(2)}) collective-permute-start(f32[1,1,8,128]{3,1,2,0:T(1,128)S(1)} %get-tuple-element.77), channel_id=1, source_target_pairs={{4,0},{8,4},{12,8},{16,12},{20,16},{24,20},{28,24},{0,28},{5,1},{9... | collective-permute-start | bytes 12296 | tf_op jit(solution)/shard_map/ppermute | solution.py:34
  8.8 0.6 copy-done.10
  9.6 0.6 collective-permute-done
  10.1 5.0 %collective-permute-done.1 = f32[1,1,8,128]{3,1,2,0:T(1,128)S(1)} collective-permute-done((f32[1,1,8,128]{3,1,2,0:T(1,128)S(1)}, f32[1,1,8,128]{3,1,2,0:T(1,128)S(1)}, u32[]{:S(2)}, u32[]{:S(2)}) %collective-permute-start.1) | collective-permute-done | bytes 4128 | tf_op jit(solution)/shard_map/ppermute | solution.py:33
  15.8 0.8 collective-permute-done.2
  16.6 1.8 %collective-permute-done.3 = f32[1,8,1,128]{3,1,2,0:T(8,128)S(1)} collective-permute-done((f32[1,8,1,128]{3,1,2,0:T(8,128)S(1)}, f32[1,8,1,128]{3,1,2,0:T(8,128)S(1)}, u32[]{:S(2)}, u32[]{:S(2)}) %collective-permute-start.3) | collective-permute-done | bytes 4128 | tf_op jit(solution)/shard_map/ppermute | solution.py:33
  18.6 0.7 copy-done.6
  20.7 2.0 %collective-permute-start.5 = (f32[1,1,8,128]{3,1,2,0:T(1,128)S(1)}, f32[1,1,8,128]{3,1,2,0:T(1,128)S(1)}, u32[]{:S(2)}, u32[]{:S(2)}) collective-permute-start(f32[1,1,8,128]{3,1,2,0:T(1,128)S(1)} %get-tuple-element.66), channel_id=1, source_target_pairs={{0,4},{4,8},{8,12},{12,16},{16,20},{20,24},{24,28},{28,0},{1,5},{5... | collective-permute-start | bytes 12296 | tf_op jit(solution)/shard_map/ppermute | solution.py:33
  22.8 1.6 %collective-permute-done.4 = f32[1,1,8,128]{3,1,2,0:T(1,128)S(1)} collective-permute-done((f32[1,1,8,128]{3,1,2,0:T(1,128)S(1)}, f32[1,1,8,128]{3,1,2,0:T(1,128)S(1)}, u32[]{:S(2)}, u32[]{:S(2)}) %collective-permute-start.4) | collective-permute-done | bytes 4128 | tf_op jit(solution)/shard_map/ppermute | solution.py:34
  24.3 2.8 %collective-permute-done.5 = f32[1,1,8,128]{3,1,2,0:T(1,128)S(1)} collective-permute-done((f32[1,1,8,128]{3,1,2,0:T(1,128)S(1)}, f32[1,1,8,128]{3,1,2,0:T(1,128)S(1)}, u32[]{:S(2)}, u32[]{:S(2)}) %collective-permute-start.5) | collective-permute-done | bytes 4128 | tf_op jit(solution)/shard_map/ppermute | solution.py:33
  27.3 0.5 collective-permute-start.7
  27.7 0.8 collective-permute-done.6
  28.6 1.8 %collective-permute-done.7 = f32[1,8,1,128]{3,1,2,0:T(8,128)S(1)} collective-permute-done((f32[1,8,1,128]{3,1,2,0:T(8,128)S(1)}, f32[1,8,1,128]{3,1,2,0:T(8,128)S(1)}, u32[]{:S(2)}, u32[]{:S(2)}) %collective-permute-start.7) | collective-permute-done | bytes 4128 | tf_op jit(solution)/shard_map/ppermute | solution.py:33
  32.1 2.0 %collective-permute-start.9 = (f32[1,1,8,128]{3,1,2,0:T(1,128)S(1)}, f32[1,1,8,128]{3,1,2,0:T(1,128)S(1)}, u32[]{:S(2)}, u32[]{:S(2)}) collective-permute-start(f32[1,1,8,128]{3,1,2,0:T(1,128)S(1)} %get-tuple-element.58), channel_id=1, source_target_pairs={{0,4},{4,8},{8,12},{12,16},{16,20},{20,24},{24,28},{28,0},{1,5},{5... | collective-permute-start | bytes 12296 | tf_op jit(solution)/shard_map/ppermute | solution.py:33
  34.1 1.5 %collective-permute-done.8 = f32[1,1,8,128]{3,1,2,0:T(1,128)S(1)} collective-permute-done((f32[1,1,8,128]{3,1,2,0:T(1,128)S(1)}, f32[1,1,8,128]{3,1,2,0:T(1,128)S(1)}, u32[]{:S(2)}, u32[]{:S(2)}) %collective-permute-start.8) | collective-permute-done | bytes 4128 | tf_op jit(solution)/shard_map/ppermute | solution.py:34
  35.6 2.8 %collective-permute-done.9 = f32[1,1,8,128]{3,1,2,0:T(1,128)S(1)} collective-permute-done((f32[1,1,8,128]{3,1,2,0:T(1,128)S(1)}, f32[1,1,8,128]{3,1,2,0:T(1,128)S(1)}, u32[]{:S(2)}, u32[]{:S(2)}) %collective-permute-start.9) | collective-permute-done | bytes 4128 | tf_op jit(solution)/shard_map/ppermute | solution.py:33
  39.2 0.7 collective-permute-done.10
  39.9 1.8 %collective-permute-done.11 = f32[1,8,1,128]{3,1,2,0:T(8,128)S(1)} collective-permute-done((f32[1,8,1,128]{3,1,2,0:T(8,128)S(1)}, f32[1,8,1,128]{3,1,2,0:T(8,128)S(1)}, u32[]{:S(2)}, u32[]{:S(2)}) %collective-permute-start.11) | collective-permute-done | bytes 4128 | tf_op jit(solution)/shard_map/ppermute | solution.py:33
  42.1 0.5 copy-done.8
  43.0 0.6 copy-done.11
  44.0 2.0 %collective-permute-start.13 = (f32[2,1,8,128]{3,1,2,0:T(1,128)S(1)}, f32[2,1,8,128]{3,1,2,0:T(1,128)S(1)}, u32[]{:S(2)}, u32[]{:S(2)}) collective-permute-start(f32[2,1,8,128]{3,1,2,0:T(1,128)S(1)} %get-tuple-element.34), channel_id=1, source_target_pairs={{0,4},{4,8},{8,12},{12,16},{16,20},{20,24},{24,28},{28,0},{1,5},{5... | collective-permute-start | bytes 24584 | tf_op jit(solution)/shard_map/ppermute | solution.py:33
  46.0 1.6 %collective-permute-done.12 = f32[2,1,8,128]{3,1,2,0:T(1,128)S(1)} collective-permute-done((f32[2,1,8,128]{3,1,2,0:T(1,128)S(1)}, f32[2,1,8,128]{3,1,2,0:T(1,128)S(1)}, u32[]{:S(2)}, u32[]{:S(2)}) %collective-permute-start.12) | collective-permute-done | bytes 8224 | tf_op jit(solution)/shard_map/ppermute | solution.py:34
  47.6 2.8 %collective-permute-done.13 = f32[2,1,8,128]{3,1,2,0:T(1,128)S(1)} collective-permute-done((f32[2,1,8,128]{3,1,2,0:T(1,128)S(1)}, f32[2,1,8,128]{3,1,2,0:T(1,128)S(1)}, u32[]{:S(2)}, u32[]{:S(2)}) %collective-permute-start.13) | collective-permute-done | bytes 8224 | tf_op jit(solution)/shard_map/ppermute | solution.py:33
  51.0 0.9 collective-permute-done.14
  51.9 1.8 %collective-permute-done.15 = f32[2,8,1,128]{3,1,2,0:T(8,128)S(1)} collective-permute-done((f32[2,8,1,128]{3,1,2,0:T(8,128)S(1)}, f32[2,8,1,128]{3,1,2,0:T(8,128)S(1)}, u32[]{:S(2)}, u32[]{:S(2)}) %collective-permute-start.15) | collective-permute-done | bytes 8224 | tf_op jit(solution)/shard_map/ppermute | solution.py:33
  54.8 0.6 copy-done.4
  55.8 0.7 copy-done.3
  56.8 2.0 %collective-permute-start.17 = (f32[1,1,8,128]{3,1,2,0:T(1,128)S(1)}, f32[1,1,8,128]{3,1,2,0:T(1,128)S(1)}, u32[]{:S(2)}, u32[]{:S(2)}) collective-permute-start(f32[1,1,8,128]{3,1,2,0:T(1,128)S(1)} %get-tuple-element.50), channel_id=1, source_target_pairs={{0,4},{4,8},{8,12},{12,16},{16,20},{20,24},{24,28},{28,0},{1,5},{5... | collective-permute-start | bytes 12296 | tf_op jit(solution)/shard_map/ppermute | solution.py:33
  58.8 1.6 %collective-permute-done.16 = f32[1,1,8,128]{3,1,2,0:T(1,128)S(1)} collective-permute-done((f32[1,1,8,128]{3,1,2,0:T(1,128)S(1)}, f32[1,1,8,128]{3,1,2,0:T(1,128)S(1)}, u32[]{:S(2)}, u32[]{:S(2)}) %collective-permute-start.16) | collective-permute-done | bytes 4128 | tf_op jit(solution)/shard_map/ppermute | solution.py:34
  60.4 2.8 %collective-permute-done.17 = f32[1,1,8,128]{3,1,2,0:T(1,128)S(1)} collective-permute-done((f32[1,1,8,128]{3,1,2,0:T(1,128)S(1)}, f32[1,1,8,128]{3,1,2,0:T(1,128)S(1)}, u32[]{:S(2)}, u32[]{:S(2)}) %collective-permute-start.17) | collective-permute-done | bytes 4128 | tf_op jit(solution)/shard_map/ppermute | solution.py:33
  63.8 0.8 collective-permute-done.18
  64.6 1.8 %collective-permute-done.19 = f32[1,8,1,128]{3,1,2,0:T(8,128)S(1)} collective-permute-done((f32[1,8,1,128]{3,1,2,0:T(8,128)S(1)}, f32[1,8,1,128]{3,1,2,0:T(8,128)S(1)}, u32[]{:S(2)}, u32[]{:S(2)}) %collective-permute-start.19) | collective-permute-done | bytes 4128 | tf_op jit(solution)/shard_map/ppermute | solution.py:33
  66.6 0.7 fusion.105
  67.3 17.8 %all-reduce.1 = (f32[]{:T(128)}, f32[]{:T(128)}) all-reduce(f32[]{:T(128)} %get-tuple-element.9, f32[]{:T(128)} %get-tuple-element.8), channel_id=1, replica_groups=mesh['dom'=8,'sub'=4] {'dom'}, use_global_device_ids=true, to_apply=%region_1.2 | all-reduce | flops 2 | bytes 16 | tf_op jit(solution)/shard_map/psum | solution.py:136
  85.1 6.3 %all-reduce.3 = (f32[]{:T(128)}, f32[]{:T(128)}) all-reduce(f32[]{:T(128)} %get-tuple-element.12, f32[]{:T(128)} %get-tuple-element.13), channel_id=1, replica_groups=mesh['dom'=8,'sub'=4] {'sub'}, use_global_device_ids=true, to_apply=%region_2.3 | all-reduce | flops 2 | bytes 16 | tf_op jit(solution)/shard_map/psum | solution.py:135
  94.0 2.1 %collective-permute-start.20 = (f32[1,1,8,128]{3,1,2,0:T(1,128)S(1)}, f32[1,1,8,128]{3,1,2,0:T(1,128)S(1)}, u32[]{:S(2)}, u32[]{:S(2)}) collective-permute-start(f32[1,1,8,128]{3,1,2,0:T(1,128)S(1)} %get-tuple-element.41), channel_id=1, source_target_pairs={{4,0},{8,4},{12,8},{16,12},{20,16},{24,20},{28,24},{0,28},{5,1},{9... | collective-permute-start | bytes 12296 | tf_op jit(solution)/shard_map/ppermute | solution.py:34
  96.1 1.5 %collective-permute-done.20 = f32[1,1,8,128]{3,1,2,0:T(1,128)S(1)} collective-permute-done((f32[1,1,8,128]{3,1,2,0:T(1,128)S(1)}, f32[1,1,8,128]{3,1,2,0:T(1,128)S(1)}, u32[]{:S(2)}, u32[]{:S(2)}) %collective-permute-start.20) | collective-permute-done | bytes 4128 | tf_op jit(solution)/shard_map/ppermute | solution.py:34
  97.7 4.7 %collective-permute-done.21 = f32[1,1,8,128]{3,1,2,0:T(1,128)S(1)} collective-permute-done((f32[1,1,8,128]{3,1,2,0:T(1,128)S(1)}, f32[1,1,8,128]{3,1,2,0:T(1,128)S(1)}, u32[]{:S(2)}, u32[]{:S(2)}) %collective-permute-start.21) | collective-permute-done | bytes 4128 | tf_op jit(solution)/shard_map/ppermute | solution.py:33
  102.5 0.5 collective-permute-start.23
  103.0 0.6 copy.103
  103.8 1.8 %collective-permute-done.23 = f32[1,8,1,128]{3,1,2,0:T(8,128)S(1)} collective-permute-done((f32[1,8,1,128]{3,1,2,0:T(8,128)S(1)}, f32[1,8,1,128]{3,1,2,0:T(8,128)S(1)}, u32[]{:S(2)}, u32[]{:S(2)}) %collective-permute-start.23) | collective-permute-done | bytes 4128 | tf_op jit(solution)/shard_map/ppermute | solution.py:33
  105.9 0.8 fusion.107
  106.7 17.8 %all-reduce = (f32[]{:T(128)}, f32[]{:T(128)}) all-reduce(f32[]{:T(128)} %get-tuple-element.7, f32[]{:T(128)} %get-tuple-element.6), channel_id=1, replica_groups=mesh['dom'=8,'sub'=4] {'dom'}, use_global_device_ids=true, to_apply=%region_7.8 | all-reduce | flops 2 | bytes 16 | tf_op jit(solution)/shard_map/psum | solution.py:136
  124.5 6.3 %all-reduce.2 = (f32[]{:T(128)}, f32[]{:T(128)}) all-reduce(f32[]{:T(128)} %get-tuple-element.10, f32[]{:T(128)} %get-tuple-element.11), channel_id=1, replica_groups=mesh['dom'=8,'sub'=4] {'sub'}, use_global_device_ids=true, to_apply=%region_8.9 | all-reduce | flops 2 | bytes 16 | tf_op jit(solution)/shard_map/psum | solution.py:135
  135.4 0.6 copy.105
  136.1 0.6 copy.104
  (122 shorter events, 11.8 us)
Async XLA Ops:
  0.6 0.8 copy-start.1
  0.6 0.8 copy-start.2
  1.6 0.8 copy-start
  2.7 7.4 %collective-permute-start = (f32[1,1,8,128]{3,1,2,0:T(1,128)S(1)}, f32[1,1,8,128]{3,1,2,0:T(1,128)S(1)}, u32[]{:S(2)}, u32[]{:S(2)}) collective-permute-start(f32[1,1,8,128]{3,1,2,0:T(1,128)S(1)} %get-tuple-element.77), channel_id=1, source_target_pairs={{4,0},{8,4},{12,8},{16,12},{20,16},{24,20},{28,24},{0,28},{5,1},{9... | collective-permute-start | bytes 12296 | tf_op jit(solution)/shard_map/ppermute | solution.py:34
  8.8 6.3 %collective-permute-start.1 = (f32[1,1,8,128]{3,1,2,0:T(1,128)S(1)}, f32[1,1,8,128]{3,1,2,0:T(1,128)S(1)}, u32[]{:S(2)}, u32[]{:S(2)}) collective-permute-start(f32[1,1,8,128]{3,1,2,0:T(1,128)S(1)} %get-tuple-element.78), channel_id=1, source_target_pairs={{0,4},{4,8},{8,12},{12,16},{16,20},{20,24},{24,28},{28,0},{1,5},{5... | collective-permute-start | bytes 12296 | tf_op jit(solution)/shard_map/ppermute | solution.py:33
  8.8 0.7 copy-start.10
  15.2 1.4 %collective-permute-start.2 = (f32[1,8,1,128]{3,1,2,0:T(8,128)S(1)}, f32[1,8,1,128]{3,1,2,0:T(8,128)S(1)}, u32[]{:S(2)}, u32[]{:S(2)}) collective-permute-start(f32[1,8,1,128]{3,1,2,0:T(8,128)S(1)} %get-tuple-element.75), channel_id=1, source_target_pairs={{1,0},{2,1},{3,2},{0,3},{5,4},{6,5},{7,6},{4,7},{9,8},{10,9},{11,1... | collective-permute-start | bytes 12296 | tf_op jit(solution)/shard_map/ppermute | solution.py:34
  15.3 3.1 %collective-permute-start.3 = (f32[1,8,1,128]{3,1,2,0:T(8,128)S(1)}, f32[1,8,1,128]{3,1,2,0:T(8,128)S(1)}, u32[]{:S(2)}, u32[]{:S(2)}) collective-permute-start(f32[1,8,1,128]{3,1,2,0:T(8,128)S(1)} %get-tuple-element.76), channel_id=1, source_target_pairs={{0,1},{1,2},{2,3},{3,0},{4,5},{5,6},{6,7},{7,4},{8,9},{9,10},{10,1... | collective-permute-start | bytes 12296 | tf_op jit(solution)/shard_map/ppermute | solution.py:33
  18.6 0.7 copy-start.6
  20.7 3.7 %collective-permute-start.4 = (f32[1,1,8,128]{3,1,2,0:T(1,128)S(1)}, f32[1,1,8,128]{3,1,2,0:T(1,128)S(1)}, u32[]{:S(2)}, u32[]{:S(2)}) collective-permute-start(f32[1,1,8,128]{3,1,2,0:T(1,128)S(1)} %get-tuple-element.65), channel_id=1, source_target_pairs={{4,0},{8,4},{12,8},{16,12},{20,16},{24,20},{28,24},{0,28},{5,1},{9... | collective-permute-start | bytes 12296 | tf_op jit(solution)/shard_map/ppermute | solution.py:34
  20.7 6.4 %collective-permute-start.5 = (f32[1,1,8,128]{3,1,2,0:T(1,128)S(1)}, f32[1,1,8,128]{3,1,2,0:T(1,128)S(1)}, u32[]{:S(2)}, u32[]{:S(2)}) collective-permute-start(f32[1,1,8,128]{3,1,2,0:T(1,128)S(1)} %get-tuple-element.66), channel_id=1, source_target_pairs={{0,4},{4,8},{8,12},{12,16},{16,20},{20,24},{24,28},{28,0},{1,5},{5... | collective-permute-start | bytes 12296 | tf_op jit(solution)/shard_map/ppermute | solution.py:33
  27.2 1.4 %collective-permute-start.6 = (f32[1,8,1,128]{3,1,2,0:T(8,128)S(1)}, f32[1,8,1,128]{3,1,2,0:T(8,128)S(1)}, u32[]{:S(2)}, u32[]{:S(2)}) collective-permute-start(f32[1,8,1,128]{3,1,2,0:T(8,128)S(1)} %get-tuple-element.63), channel_id=1, source_target_pairs={{1,0},{2,1},{3,2},{0,3},{5,4},{6,5},{7,6},{4,7},{9,8},{10,9},{11,1... | collective-permute-start | bytes 12296 | tf_op jit(solution)/shard_map/ppermute | solution.py:34
  27.3 3.1 %collective-permute-start.7 = (f32[1,8,1,128]{3,1,2,0:T(8,128)S(1)}, f32[1,8,1,128]{3,1,2,0:T(8,128)S(1)}, u32[]{:S(2)}, u32[]{:S(2)}) collective-permute-start(f32[1,8,1,128]{3,1,2,0:T(8,128)S(1)} %get-tuple-element.64), channel_id=1, source_target_pairs={{0,1},{1,2},{2,3},{3,0},{4,5},{5,6},{6,7},{7,4},{8,9},{9,10},{10,1... | collective-permute-start | bytes 12296 | tf_op jit(solution)/shard_map/ppermute | solution.py:33
  32.0 2.1 %copy-start.9 = (f32[8]{0:T(128)S(1)}, f32[8]{0:T(128)}, u32[]{:S(2)}) copy-start(f32[8]{0:T(128)} %constant.109.clone) | copy-start | bytes 100
  32.0 3.7 %collective-permute-start.8 = (f32[1,1,8,128]{3,1,2,0:T(1,128)S(1)}, f32[1,1,8,128]{3,1,2,0:T(1,128)S(1)}, u32[]{:S(2)}, u32[]{:S(2)}) collective-permute-start(f32[1,1,8,128]{3,1,2,0:T(1,128)S(1)} %get-tuple-element.57), channel_id=1, source_target_pairs={{4,0},{8,4},{12,8},{16,12},{20,16},{24,20},{28,24},{0,28},{5,1},{9... | collective-permute-start | bytes 12296 | tf_op jit(solution)/shard_map/ppermute | solution.py:34
  32.1 6.4 %collective-permute-start.9 = (f32[1,1,8,128]{3,1,2,0:T(1,128)S(1)}, f32[1,1,8,128]{3,1,2,0:T(1,128)S(1)}, u32[]{:S(2)}, u32[]{:S(2)}) collective-permute-start(f32[1,1,8,128]{3,1,2,0:T(1,128)S(1)} %get-tuple-element.58), channel_id=1, source_target_pairs={{0,4},{4,8},{8,12},{12,16},{16,20},{20,24},{24,28},{28,0},{1,5},{5... | collective-permute-start | bytes 12296 | tf_op jit(solution)/shard_map/ppermute | solution.py:33
  34.1 4.9 %copy-start.5 = (f32[8,8,128]{2,1,0:T(8,128)S(1)}, f32[8,8,128]{2,1,0:T(8,128)}, u32[]{:S(2)}) copy-start(f32[8,8,128]{2,1,0:T(8,128)} %param.41) | copy-start | bytes 98308
  38.5 0.7 copy-start.7
  38.5 1.4 %collective-permute-start.10 = (f32[1,8,1,128]{3,1,2,0:T(8,128)S(1)}, f32[1,8,1,128]{3,1,2,0:T(8,128)S(1)}, u32[]{:S(2)}, u32[]{:S(2)}) collective-permute-start(f32[1,8,1,128]{3,1,2,0:T(8,128)S(1)} %get-tuple-element.55), channel_id=1, source_target_pairs={{1,0},{2,1},{3,2},{0,3},{5,4},{6,5},{7,6},{4,7},{9,8},{10,9},{11,1... | collective-permute-start | bytes 12296 | tf_op jit(solution)/shard_map/ppermute | solution.py:34
  38.6 3.1 %collective-permute-start.11 = (f32[1,8,1,128]{3,1,2,0:T(8,128)S(1)}, f32[1,8,1,128]{3,1,2,0:T(8,128)S(1)}, u32[]{:S(2)}, u32[]{:S(2)}) collective-permute-start(f32[1,8,1,128]{3,1,2,0:T(8,128)S(1)} %get-tuple-element.56), channel_id=1, source_target_pairs={{0,1},{1,2},{2,3},{3,0},{4,5},{5,6},{6,7},{7,4},{8,9},{9,10},{10,1... | collective-permute-start | bytes 12296 | tf_op jit(solution)/shard_map/ppermute | solution.py:33
  41.9 0.7 copy-start.8
  42.8 0.8 copy-start.11
  43.9 3.7 %collective-permute-start.12 = (f32[2,1,8,128]{3,1,2,0:T(1,128)S(1)}, f32[2,1,8,128]{3,1,2,0:T(1,128)S(1)}, u32[]{:S(2)}, u32[]{:S(2)}) collective-permute-start(f32[2,1,8,128]{3,1,2,0:T(1,128)S(1)} %get-tuple-element.33), channel_id=1, source_target_pairs={{4,0},{8,4},{12,8},{16,12},{20,16},{24,20},{28,24},{0,28},{5,1},{9... | collective-permute-start | bytes 24584 | tf_op jit(solution)/shard_map/ppermute | solution.py:34
  44.0 6.4 %collective-permute-start.13 = (f32[2,1,8,128]{3,1,2,0:T(1,128)S(1)}, f32[2,1,8,128]{3,1,2,0:T(1,128)S(1)}, u32[]{:S(2)}, u32[]{:S(2)}) collective-permute-start(f32[2,1,8,128]{3,1,2,0:T(1,128)S(1)} %get-tuple-element.34), channel_id=1, source_target_pairs={{0,4},{4,8},{8,12},{12,16},{16,20},{20,24},{24,28},{28,0},{1,5},{5... | collective-permute-start | bytes 24584 | tf_op jit(solution)/shard_map/ppermute | solution.py:33
  50.5 1.4 %collective-permute-start.14 = (f32[2,8,1,128]{3,1,2,0:T(8,128)S(1)}, f32[2,8,1,128]{3,1,2,0:T(8,128)S(1)}, u32[]{:S(2)}, u32[]{:S(2)}) collective-permute-start(f32[2,8,1,128]{3,1,2,0:T(8,128)S(1)} %get-tuple-element.31), channel_id=1, source_target_pairs={{1,0},{2,1},{3,2},{0,3},{5,4},{6,5},{7,6},{4,7},{9,8},{10,9},{11,1... | collective-permute-start | bytes 24584 | tf_op jit(solution)/shard_map/ppermute | solution.py:34
  50.5 3.2 %collective-permute-start.15 = (f32[2,8,1,128]{3,1,2,0:T(8,128)S(1)}, f32[2,8,1,128]{3,1,2,0:T(8,128)S(1)}, u32[]{:S(2)}, u32[]{:S(2)}) collective-permute-start(f32[2,8,1,128]{3,1,2,0:T(8,128)S(1)} %get-tuple-element.32), channel_id=1, source_target_pairs={{0,1},{1,2},{2,3},{3,0},{4,5},{5,6},{6,7},{7,4},{8,9},{9,10},{10,1... | collective-permute-start | bytes 24584 | tf_op jit(solution)/shard_map/ppermute | solution.py:33
  54.7 0.7 copy-start.4
  55.6 0.9 copy-start.3
  56.7 3.7 %collective-permute-start.16 = (f32[1,1,8,128]{3,1,2,0:T(1,128)S(1)}, f32[1,1,8,128]{3,1,2,0:T(1,128)S(1)}, u32[]{:S(2)}, u32[]{:S(2)}) collective-permute-start(f32[1,1,8,128]{3,1,2,0:T(1,128)S(1)} %get-tuple-element.49), channel_id=1, source_target_pairs={{4,0},{8,4},{12,8},{16,12},{20,16},{24,20},{28,24},{0,28},{5,1},{9... | collective-permute-start | bytes 12296 | tf_op jit(solution)/shard_map/ppermute | solution.py:34
  56.8 6.4 %collective-permute-start.17 = (f32[1,1,8,128]{3,1,2,0:T(1,128)S(1)}, f32[1,1,8,128]{3,1,2,0:T(1,128)S(1)}, u32[]{:S(2)}, u32[]{:S(2)}) collective-permute-start(f32[1,1,8,128]{3,1,2,0:T(1,128)S(1)} %get-tuple-element.50), channel_id=1, source_target_pairs={{0,4},{4,8},{8,12},{12,16},{16,20},{20,24},{24,28},{28,0},{1,5},{5... | collective-permute-start | bytes 12296 | tf_op jit(solution)/shard_map/ppermute | solution.py:33
  63.2 1.4 %collective-permute-start.18 = (f32[1,8,1,128]{3,1,2,0:T(8,128)S(1)}, f32[1,8,1,128]{3,1,2,0:T(8,128)S(1)}, u32[]{:S(2)}, u32[]{:S(2)}) collective-permute-start(f32[1,8,1,128]{3,1,2,0:T(8,128)S(1)} %get-tuple-element.47), channel_id=1, source_target_pairs={{1,0},{2,1},{3,2},{0,3},{5,4},{6,5},{7,6},{4,7},{9,8},{10,9},{11,1... | collective-permute-start | bytes 12296 | tf_op jit(solution)/shard_map/ppermute | solution.py:34
  63.3 3.1 %collective-permute-start.19 = (f32[1,8,1,128]{3,1,2,0:T(8,128)S(1)}, f32[1,8,1,128]{3,1,2,0:T(8,128)S(1)}, u32[]{:S(2)}, u32[]{:S(2)}) collective-permute-start(f32[1,8,1,128]{3,1,2,0:T(8,128)S(1)} %get-tuple-element.48), channel_id=1, source_target_pairs={{0,1},{1,2},{2,3},{3,0},{4,5},{5,6},{6,7},{7,4},{8,9},{9,10},{10,1... | collective-permute-start | bytes 12296 | tf_op jit(solution)/shard_map/ppermute | solution.py:33
  94.0 3.7 %collective-permute-start.20 = (f32[1,1,8,128]{3,1,2,0:T(1,128)S(1)}, f32[1,1,8,128]{3,1,2,0:T(1,128)S(1)}, u32[]{:S(2)}, u32[]{:S(2)}) collective-permute-start(f32[1,1,8,128]{3,1,2,0:T(1,128)S(1)} %get-tuple-element.41), channel_id=1, source_target_pairs={{4,0},{8,4},{12,8},{16,12},{20,16},{24,20},{28,24},{0,28},{5,1},{9... | collective-permute-start | bytes 12296 | tf_op jit(solution)/shard_map/ppermute | solution.py:34
  96.1 6.3 %collective-permute-start.21 = (f32[1,1,8,128]{3,1,2,0:T(1,128)S(1)}, f32[1,1,8,128]{3,1,2,0:T(1,128)S(1)}, u32[]{:S(2)}, u32[]{:S(2)}) collective-permute-start(f32[1,1,8,128]{3,1,2,0:T(1,128)S(1)} %get-tuple-element.42), channel_id=1, source_target_pairs={{0,4},{4,8},{8,12},{12,16},{16,20},{20,24},{24,28},{28,0},{1,5},{5... | collective-permute-start | bytes 12296 | tf_op jit(solution)/shard_map/ppermute | solution.py:33
  102.4 1.4 %collective-permute-start.22 = (f32[1,8,1,128]{3,1,2,0:T(8,128)S(1)}, f32[1,8,1,128]{3,1,2,0:T(8,128)S(1)}, u32[]{:S(2)}, u32[]{:S(2)}) collective-permute-start(f32[1,8,1,128]{3,1,2,0:T(8,128)S(1)} %get-tuple-element.39), channel_id=1, source_target_pairs={{1,0},{2,1},{3,2},{0,3},{5,4},{6,5},{7,6},{4,7},{9,8},{10,9},{11,1... | collective-permute-start | bytes 12296 | tf_op jit(solution)/shard_map/ppermute | solution.py:34
  102.5 3.1 %collective-permute-start.23 = (f32[1,8,1,128]{3,1,2,0:T(8,128)S(1)}, f32[1,8,1,128]{3,1,2,0:T(8,128)S(1)}, u32[]{:S(2)}, u32[]{:S(2)}) collective-permute-start(f32[1,8,1,128]{3,1,2,0:T(8,128)S(1)} %get-tuple-element.40), channel_id=1, source_target_pairs={{0,1},{1,2},{2,3},{3,0},{4,5},{5,6},{6,7},{7,4},{8,9},{9,10},{10,1... | collective-permute-start | bytes 12296 | tf_op jit(solution)/shard_map/ppermute | solution.py:33
